TPU v7x, 16 devices: a whole 2x2x2 slice. The times are simulated.
16 devices in a mesh: data: 4 (over z, y), model: 4 (over x, core).
Axes of the slice: x: 2, y: 2, z: 2, core: 2. Of those that a mesh axis runs over, the one named last changes fastest.
Arguments:
- hidden: bfloat16 [8192, 6144], P('data', 'model')
- unembed: bfloat16 [50432, 6144], P('model', 'data')
- draft_ids: int32 [8192], P('data')
- q_prob: float32 [8192], P('data')
Outputs:
- output 1: float32 [8192], P('data')
- output 2: float32 [8192], P('data')
All inputs are finite; a program needn't handle non-finite values.
Results may differ from a plain program's by a relative error of at most 0.001.
Values are sent between devices in bfloat16 or wider.
A program may use at most 1 GiB of HBM per device.

v0:
```python
import jax
import jax.numpy as jnp
from jax import lax
from jax.sharding import PartitionSpec as P


def solution(mesh):
    def per_device(h_part, w_part, draft_loc, q_loc):
        h_rows = lax.all_gather(h_part, "model", axis=1, tiled=True)
        w_rows = lax.all_gather(w_part, "data", axis=1, tiled=True)
        logits = lax.dot_general(h_rows, w_rows, (((1,), (1,)), ((), ())), preferred_element_type=jnp.float32)
        shard_vocab = w_rows.shape[0]
        row_max = lax.pmax(jnp.max(logits, axis=1), "model")
        local_sum = jnp.sum(jnp.exp(logits - row_max[:, None]), axis=1)
        vocab_ids = lax.axis_index("model") * shard_vocab + lax.broadcasted_iota(jnp.int32, (1, shard_vocab), 1)
        local_pick = jnp.sum(jnp.where(vocab_ids == draft_loc[:, None], logits, 0.0), axis=1)
        totals = lax.psum(jnp.stack([local_sum, local_pick]), "model")
        log_prob = totals[1] - row_max - jnp.log(totals[0])
        accept = jnp.minimum(1.0, jnp.exp(log_prob) / q_loc)
        return log_prob, accept

    return jax.shard_map(per_device, mesh=mesh, in_specs=(P("data", "model"), P("model", "data"), P("data"), P("data")), out_specs=(P("data"), P("data")), check_vma=False)
```

profile of v0, /device:TPU:0, one launch (start us, length us, event | category | flops | bytes accessed | tf_op | source)
XLA Modules:
  0.0 1870.2 jit_solution(14386323767918120942)
XLA Ops:
  7.2 0.0 all-gather.3.cloned.1.call-start
  7.2 0.7 all-gather.3.cloned.1.call-update
  7.9 0.0 all-gather.5.cloned.1.call-start
  7.9 0.7 all-gather.5.cloned.1.call-update
  8.7 0.6 iota_add_fusion
  9.3 156.8 %all-gather.3.cloned.1.call-done = bf16[2048,6144]{1,0:T(8,128)(2,1)} async-done(((bf16[2048,1536]{1,0:T(8,128)(2,1)}), bf16[2048,6144]{1,0:T(8,128)(2,1)}) %all-gather.3.cloned.1.call-update) | async-done | bytes 25165840 | tf_op jit(solution)/shard_map/all_gather | solution.py:9
  166.1 1307.0 %all-gather.5.cloned.1.call-done = bf16[12608,6144]{1,0:T(8,128)(2,1)} async-done(((bf16[12608,1536]{1,0:T(8,128)(2,1)}), bf16[12608,6144]{1,0:T(8,128)(2,1)}) %all-gather.5.cloned.1.call-update) | async-done | bytes 154927120 | tf_op jit(solution)/shard_map/all_gather | solution.py:10
  1473.1 0.0 copy-start
  1473.1 0.0 copy-start.1
  1473.1 337.8 %fusion.1 = (f32[2048]{0:T(1024)S(1)}, f32[2048,12608]{0,1:T(8,128)}) fusion(bf16[2048,6144]{1,0:T(8,128)(2,1)} %all-gather.3.cloned.1.call-done, bf16[12608,6144]{1,0:T(8,128)(2,1)} %all-gather.5.cloned.1.call-done), kind=kOutput, calls=%fused_computation.8 | convolution fusion | flops 317316530176 | bytes 283385856 | tf_op jit(solution)/shard_map/dot_general | solution.py:11
  1810.9 0.0 copy-start.2
  1810.9 6.4 pmax.7
  1817.3 0.0 copy-done
  1817.3 0.0 copy-done.1
  1817.4 35.1 %exponential_reduce_fusion = (f32[2048]{0:T(1024)S(1)}, f32[2048]{0:T(1024)S(1)}) fusion(f32[2048,12608]{0,1:T(8,128)} %get-tuple-element.9, f32[2048]{0:T(1024)S(1)} %pmax.7, s32[2048]{0:T(1024)S(1)} %copy-done.1, s32[12608]{0:T(1024)S(1)} %copy-done), kind=kLoop, calls=%fused_computation.1 | loop fusion | flops 129101824 | bytes 103367936 | tf_op jit(solution)/shard_map/reduce_sum | solution.py:14
  1852.5 10.2 psum.7
  1862.7 0.0 copy-done.2
  1862.8 0.6 divide_minimum_fusion
  (2 shorter events, 0.0 us)
Async XLA Ops:
  7.2 159.0 %all-gather.3.cloned.1.call-start = ((), (), s32[]{:S(2)}) async-start(), calls=%async_computation | async-start | bytes 31457280 | tf_op jit(solution)/shard_map/all_gather | solution.py:9
  7.9 1465.2 %all-gather.5.cloned.1.call-start = ((), (), s32[]{:S(2)}) async-start(), calls=%async_computation.1 | async-start | bytes 193658880 | tf_op jit(solution)/shard_map/all_gather | solution.py:10
  1473.1 344.2 %copy-start = (s32[12608]{0:T(1024)S(1)}, s32[12608]{0:T(1024)}, u32[]{:S(2)}) copy-start(s32[12608]{0:T(1024)} %iota_add_fusion) | copy-start | bytes 151300
  1473.1 344.2 %copy-start.1 = (s32[2048]{0:T(1024)S(1)}, s32[2048]{0:T(1024)}, u32[]{:S(2)}) copy-start(s32[2048]{0:T(1024)} %param.6) | copy-start | bytes 24580
  1810.9 51.8 %copy-start.2 = (f32[2048]{0:T(1024)S(1)}, f32[2048]{0:T(1024)}, u32[]{:S(2)}) copy-start(f32[2048]{0:T(1024)} %param.7) | copy-start | bytes 24580
Sparse Core Ops, SparseCore 0:
  9.5 156.5 all-gather.2
  167.9 1305.1 all-gather.4
where the time goes:
time: 1870 us
  waiting for transfers between devices  1470 us (79%)
  matrix products  338 us (18%)
  other arithmetic  36.3 us (2%)
    all_gather x1, waiting for transfers between devices, per_device(): w_rows = lax.all_gather(w_part, 'data', axis=1, tiled=True)  1310 us
    dot_general x1, matrix products, per_device(): lax.dot_general(h_rows, w_rows, (((1,), (1,)), ((), ())), preferred_eleme...  338 us
    all_gather x1, waiting for transfers between devices, per_device(): h_rows = lax.all_gather(h_part, 'model', axis=1, tiled=True)  157 us
  transfers between devices with their start and end apart: 2, of which 2 were waited for; matrix products, arithmetic and copies ran while one was open for 0% of the time, Pallas kernels for 0%

commit v1 on v0

v1 whole, which is shorter than its diff:
```python
import functools

import jax
import jax.numpy as jnp
from jax import lax
from jax.experimental import pallas as pl
from jax.experimental.pallas import tpu as pltpu
from jax.sharding import PartitionSpec as P

MESH = pl.DeviceIdType.MESH
SUBS = 4
TILES = 16
X_STEP = 34.0
W_TIMES = (87.0, 174.0, 261.0, 382.0, 469.0, 522.0, 575.0, 620.0)


def tile_of(q):
    if q < 4:
        return 0, q
    if q < 12:
        return 1 + q % 2, (q - 4) // 2
    return 3, q - 12


def plan(n_chunks):
    items = []
    w_times = [W_TIMES[-1] * (j + 1) / n_chunks for j in range(n_chunks)] if n_chunks != len(W_TIMES) else W_TIMES
    for q in range(TILES):
        items.append((X_STEP * (q + 1), 0, ("x", q)))
        items.append((X_STEP * (q + 1) + 4.0, 2, ("h", q)))
    for i, t in enumerate((34.0, 121.0, 208.0, 329.0)):
        items.append((t, 1, ("yz", i)))
    for i, t in enumerate((330.0, 331.0, 416.0, 417.0)):
        items.append((t, 1, ("diag", i)))
    for j in range(n_chunks):
        items.append((w_times[j], 3, ("w", j)))
    items.sort()
    runs, events, n_h, n_w = [], [], 0, 0
    for _, _, (kind, k) in items:
        events.append((kind, k))
        if kind == "h":
            if n_w:
                runs.append((events, (k, 0, 0, 1, n_w)))
                events = []
            n_h += 1
        if kind == "w":
            if n_h:
                runs.append((events, (0, 1, k, 0, n_h)))
                events = []
            n_w += 1
    assert not events
    return runs


def kernel(
    v_tile, h_ref, w_ref, ids_ref, q_ref, lp_ref, acc_ref, hbuf,
    wv, hv, ids_all, mx, sm, pk, st_send, st_recv,
    ss, rs, wss, wrs, wls, iss, irs, ils, sss, srs, lsem,
):
    rows, kp = h_ref.shape
    tile = rows // SUBS
    vocab = w_ref.shape[0]
    share = vocab // 4
    n_chunks = -(-share // v_tile)
    runs = plan(n_chunks)

    d, m = lax.axis_index("data"), lax.axis_index("model")
    y, z = lax.rem(d, 2), d // 2
    core, x = lax.rem(m, 2), m // 2
    m_sib = m + 1 - 2 * core
    m_x = m + 2 - 4 * x
    m_xs = m_sib + 2 - 4 * x

    def block(rb):
        ry, rz = rb % 2, rb // 2
        yy = 1 - y if ry else y
        zz = 1 - z if rz else z
        return zz * 2 + yy

    def row0(q):
        rb, sub = tile_of(q)
        return pl.multiple_of(block(rb) * rows + sub * tile, tile)

    def own_piece(q):
        rb, sub = tile_of(q)
        return h_ref.at[pl.ds(sub * tile, tile), :] if rb == 0 else hbuf.at[m, pl.ds(row0(q), tile), :]

    def send_h(src, q_here, q_there, mm, dev, sem):
        return pltpu.make_async_remote_copy(
            src_ref=src, dst_ref=hbuf.at[mm, pl.ds(row0(q_here), tile), :], send_sem=ss.at[sem],
            recv_sem=rs.at[q_there * 4 + mm], device_id=dev, device_id_type=MESH)

    def wait_h(q, mm):
        pltpu.make_async_remote_copy(
            src_ref=hbuf.at[mm, pl.ds(row0(q), tile), :], dst_ref=hbuf.at[mm, pl.ds(row0(q), tile), :],
            send_sem=ss.at[0], recv_sem=rs.at[q * 4 + mm], device_id=(d, m), device_id_type=MESH).wait_recv()

    def w_size(j):
        return min(v_tile, share - j * v_tile)

    def send_w(j, rb):
        size, dd = w_size(j), block(rb)
        return pltpu.make_async_remote_copy(
            src_ref=w_ref.at[pl.ds(pl.multiple_of(dd * share + j * v_tile, 8), size), :],
            dst_ref=wv.at[pl.ds(j * v_tile, size), pl.ds(pl.multiple_of(d * kp, kp), kp)],
            send_sem=wss.at[j * 4 + rb], recv_sem=wrs.at[j * 4 + rb], device_id=(dd, m), device_id_type=MESH)

    def wait_w(j, rb):
        size, dd = w_size(j), block(rb)
        pltpu.make_async_remote_copy(
            src_ref=w_ref.at[pl.ds(0, size), :],
            dst_ref=wv.at[pl.ds(j * v_tile, size), pl.ds(pl.multiple_of(dd * kp, kp), kp)],
            send_sem=wss.at[j * 4 + rb], recv_sem=wrs.at[j * 4 + rb], device_id=(d, m), device_id_type=MESH).wait_recv()

    def local_w(j):
        size = w_size(j)
        return pltpu.make_async_copy(
            w_ref.at[pl.ds(pl.multiple_of(d * share + j * v_tile, 8), size), :],
            wv.at[pl.ds(j * v_tile, size), pl.ds(pl.multiple_of(d * kp, kp), kp)], wls.at[j])

    def send_ids(rb):
        return pltpu.make_async_remote_copy(
            src_ref=ids_ref, dst_ref=ids_all.at[rb], send_sem=iss.at[rb], recv_sem=irs.at[rb],
            device_id=(block(rb), m), device_id_type=MESH)

    def over_y(i):
        send_h(own_piece(i), i, 4 + 2 * i, m, (block(1), m), 48 + i).start()

    def over_z(i):
        send_h(own_piece(i), i, 5 + 2 * i, m, (block(2), m), 52 + i).start()

    def weights(j):
        if j < n_chunks:
            for rb in (3, 1, 2):
                send_w(j, rb).start()

    def spread(q):
        send_h(own_piece(q), q, q, m, (d, m_x), q).start()
        send_h(own_piece(q), q, q, m, (d, m_sib), 16 + q).start()

    def event(kind, k):
        if kind == "x":
            wait_h(k, m_x)
            send_h(hbuf.at[m_x, pl.ds(row0(k), tile), :], k, k, m_x, (d, m_sib), 32 + k).start()
        elif kind == "h":
            wait_h(k, m_sib)
            wait_h(k, m_xs)
        elif kind == "yz":
            wait_h(4 + 2 * k, m)
            wait_h(5 + 2 * k, m)
            if k % 2 == 0:
                send_h(own_piece(5 + 2 * k), 5 + 2 * k, 12 + k, m, (block(1), m), 56 + k).start()
            else:
                send_h(own_piece(4 + 2 * k), 4 + 2 * k, 12 + k, m, (block(2), m), 56 + k).start()
            spread(4 + 2 * k)
            spread(5 + 2 * k)
            if k == 1:
                over_y(3)
                over_z(3)
                weights(3)
            elif k == 2:
                weights(4)
            elif k == 3:
                for j in range(5, n_chunks):
                    weights(j)
        elif kind == "diag":
            wait_h(12 + k, m)
            spread(12 + k)
        else:
            local_w(k).wait()
            for rb in (1, 2, 3):
                wait_w(k, rb)

    def rb_sub(q):
        mid = q >= 4
        late = q >= 12
        rb = jnp.where(late, 3, jnp.where(mid, 1 + lax.rem(q, 2), 0))
        sub = jnp.where(late, q - 12, jnp.where(mid, (q - 4) // 2, q))
        return rb, sub

    def load_parts(q, slot, act):
        rb, sub = rb_sub(q)
        ry, rz = lax.rem(rb, 2), rb // 2
        yy, zz = y + ry - 2 * y * ry, z + rz - 2 * z * rz
        row = pl.multiple_of((zz * 2 + yy) * rows + sub * tile, tile)
        for mm in range(4):
            dst = hv.at[slot, :, pl.ds(mm * kp, kp)]
            mine = jnp.logical_and(rb == 0, m == mm)

            @pl.when(mine)
            def _():
                act(pltpu.make_async_copy(h_ref.at[pl.ds(pl.multiple_of(sub * tile, tile), tile), :], dst, lsem.at[slot * 4 + mm]))

            @pl.when(jnp.logical_not(mine))
            def _():
                act(pltpu.make_async_copy(hbuf.at[mm, pl.ds(row, tile), :], dst, lsem.at[slot * 4 + mm]))

    def wait_parts(slot):
        for mm in range(4):
            pltpu.make_async_copy(
                h_ref.at[pl.ds(0, tile), :], hv.at[slot, :, pl.ds(mm * kp, kp)], lsem.at[slot * 4 + mm]).wait()

    own_ids = pltpu.make_async_copy(ids_ref, ids_all.at[0], ils)
    own_ids.start()
    for rb in (1, 2, 3):
        send_ids(rb).start()
    for i in range(3):
        over_y(i)
        over_z(i)
        if i == 0:
            for q in range(4):
                spread(q)
        weights(i)
    for j in range(n_chunks):
        local_w(j).start()
    mx[...] = jnp.full(mx.shape, -jnp.inf, jnp.float32)
    sm[...] = jnp.zeros(sm.shape, jnp.float32)
    pk[...] = jnp.zeros(pk.shape, jnp.float32)
    own_ids.wait()
    for rb in (1, 2, 3):
        send_ids(rb).wait()

    first_events, first_run = runs[0]
    for e in first_events:
        event(*e)
    load_parts(jnp.int32(first_run[0]), 0, lambda c: c.start())

    base = m * vocab + d * share

    def compute(q, j, slot):
        start = pl.multiple_of(jnp.minimum(j * v_tile, share - v_tile), 8)
        skip = j * v_tile - start
        logits = lax.dot_general(
            wv[pl.ds(start, v_tile), :], hv[slot], (((1,), (1,)), ((), ())), preferred_element_type=jnp.float32)
        local = lax.broadcasted_iota(jnp.int32, (v_tile, tile), 0)
        fresh = local >= skip
        rb, sub = rb_sub(q)
        want = ids_all[rb, sub] - (base + start)
        logits = jnp.where(fresh, logits, -jnp.inf)
        hit = jnp.logical_and(fresh, local == want)
        old = mx[q]
        stack = logits.reshape(v_tile // 8, 8, tile)
        new = jnp.maximum(old, jnp.max(stack, axis=0))
        grown = jnp.sum(jnp.exp(stack - new[None]), axis=0)
        sm[q] = sm[q] * jnp.exp(old - new) + grown
        mx[q] = new
        pk[q] = pk[q] + jnp.sum(jnp.where(hit, logits, 0.0).reshape(v_tile // 8, 8, tile), axis=0)

    n_runs = len(runs)

    def pick(r, values):
        out = jnp.int32(values[0])
        for i in range(1, len(values)):
            if values[i] != values[i - 1]:
                out = jnp.where(r >= i, jnp.int32(values[i]), out)
        return out

    q0s, dqs, j0s, djs, ns = (tuple(run[i] for _, run in runs) for i in range(5))

    def run_body(r, s0):
        q0, dq, j0, dj, n = (pick(r, v) for v in (q0s, dqs, j0s, djs, ns))
        q_next = pick(r, q0s[1:] + (0,))

        def step(i, carry):
            s = s0 + i
            slot = lax.rem(s, 2)
            last = i == n - 1

            @pl.when(last)
            def _():
                for k in range(1, n_runs):
                    if runs[k][0]:
                        @pl.when(r == k - 1)
                        def _(k=k):
                            for e in runs[k][0]:
                                event(*e)

            @pl.when(jnp.logical_not(jnp.logical_and(last, r == n_runs - 1)))
            def _():
                load_parts(jnp.where(last, q_next, q0 + dq * (i + 1)), 1 - slot, lambda c: c.start())

            wait_parts(slot)
            compute(q0 + dq * i, j0 + dj * i, slot)
            return carry

        lax.fori_loop(0, n, step, 0)
        return s0 + n

    lax.fori_loop(0, n_runs, run_body, jnp.int32(0))

    lanes = 128
    for q in range(TILES):
        rb, sub = tile_of(q)
        old = mx[q]
        top = jnp.max(old, axis=0, keepdims=True)
        parts = (top, jnp.sum(sm[q] * jnp.exp(old - top), axis=0, keepdims=True), jnp.sum(pk[q], axis=0, keepdims=True))
        for k, part in enumerate(parts):
            for i in range(tile // lanes):
                st_send[rb, k, pl.ds(sub * (tile // lanes) + i, 1), :] = part[:, i * lanes:(i + 1) * lanes]

    me = d * 4 + m
    st_recv[me] = st_send[0]

    def send_stats(rb, o):
        return pltpu.make_async_remote_copy(
            src_ref=st_send.at[rb], dst_ref=st_recv.at[me], send_sem=sss.at[rb * 4 + o], recv_sem=srs.at[me],
            device_id=(block(rb), lax.rem(m + o, 4)), device_id_type=MESH)

    others = [(rb, o) for rb in (3, 2, 1, 0) for o in range(4) if (rb, o) != (0, 0)]
    for rb, o in others:
        send_stats(rb, o).start()

    def drain(i, carry):
        pltpu.make_async_remote_copy(
            src_ref=h_ref.at[pl.ds(0, tile), :], dst_ref=hbuf.at[0, pl.ds(0, tile), :], send_sem=ss.at[i],
            recv_sem=rs.at[0], device_id=(d, m), device_id_type=MESH).wait_send()
        return carry

    lax.fori_loop(0, 60, drain, 0)
    for j in range(n_chunks):
        for rb in (1, 2, 3):
            send_w(j, rb).wait_send()
    for rb, o in others:
        send_stats(rb, o).wait_send()
    for rb, o in others:
        source = block(rb) * 4 + lax.rem(m + o, 4)
        pltpu.make_async_remote_copy(
            src_ref=st_send.at[rb], dst_ref=st_recv.at[source], send_sem=sss.at[rb * 4 + o], recv_sem=srs.at[source],
            device_id=(d, m), device_id_type=MESH).wait_recv()

    top = jnp.max(st_recv[:, 0], axis=0)
    total = jnp.sum(st_recv[:, 1] * jnp.exp(st_recv[:, 0] - top[None]), axis=0)
    picked = jnp.sum(st_recv[:, 2], axis=0)
    log_prob = picked - (top + jnp.log(total))
    lp_ref[...] = log_prob
    acc_ref[...] = jnp.minimum(1.0, jnp.exp(log_prob) / q_ref[...])


def build(mesh, v_tile):
    def per_device(h_part, w_part, draft_loc, q_loc):
        rows, kp = h_part.shape
        vocab = w_part.shape[0]
        share, tile = vocab // 4, rows // SUBS
        n_chunks = -(-share // v_tile)
        lanes = 128
        flat = (rows // lanes, lanes)
        dma, vmem = pltpu.SemaphoreType.DMA, pltpu.VMEM
        any_space = pl.BlockSpec(memory_space=pl.ANY)
        in_vmem = pl.BlockSpec(memory_space=pltpu.VMEM)
        lp, acc, _ = pl.pallas_call(
            functools.partial(kernel, v_tile),
            out_shape=(
                jax.ShapeDtypeStruct(flat, jnp.float32),
                jax.ShapeDtypeStruct(flat, jnp.float32),
                jax.ShapeDtypeStruct((4, 4 * rows, kp), jnp.bfloat16),
            ),
            in_specs=[any_space, any_space, in_vmem, in_vmem],
            out_specs=(in_vmem, in_vmem, any_space),
            scratch_shapes=[
                vmem((share, 4 * kp), jnp.bfloat16),
                vmem((2, tile, 4 * kp), jnp.bfloat16),
                vmem((4, SUBS, 1, tile), jnp.int32),
                vmem((TILES, 8, tile), jnp.float32),
                vmem((TILES, 8, tile), jnp.float32),
                vmem((TILES, 8, tile), jnp.float32),
                vmem((4, 3) + flat, jnp.float32),
                vmem((16, 3) + flat, jnp.float32),
                dma((60,)), dma((64,)), dma((4 * n_chunks,)), dma((4 * n_chunks,)), dma((n_chunks,)),
                dma((4,)), dma((4,)), dma, dma((16,)), dma((16,)), dma((8,)),
            ],
            compiler_params=pltpu.CompilerParams(has_side_effects=True, vmem_limit_bytes=66_000_000),
            name="head",
        )(h_part, w_part, draft_loc.reshape(SUBS, 1, tile), q_loc.reshape(flat))
        return lp.reshape(rows), acc.reshape(rows)

    return jax.shard_map(
        per_device, mesh=mesh, in_specs=(P("data", "model"), P("model", "data"), P("data"), P("data")),
        out_specs=(P("data"), P("data")), check_vma=False)


def solution(mesh):
    return build(mesh, 400)
```

time: 1870 us -> 761 us (0.41)
  waiting for transfers between devices: 1470 us -> 0 us
  Pallas kernels: 0 us -> 757 us
  matrix products: 338 us -> 0 us
  other arithmetic: 36.3 us -> 0 us
    all_gather x2 -> x0, waiting for transfers between devices: 1460 us -> none  [the longest x1 1310 us: per_device(): w_rows = lax.all_gather(w_part, 'data', axis=1, tiled=True)]
    pallas_call x0 -> x1, Pallas kernels: none -> 757 us  [per_device(): pl.pallas_call(functools.partial(kernel, v_tile), out_shape=(jax.ShapeDty...]
    dot_general x1 -> x0, matrix products: 338 us -> none  [per_device(): lax.dot_general(h_rows, w_rows, (((1,), (1,)), ((), ())), preferred_eleme...]
    reduce_sum x1 -> x0, other arithmetic: 35.1 us -> none  [per_device(): local_sum = jnp.sum(jnp.exp(logits - row_max[:, None]), axis=1)]
  transfers between devices with their start and end apart: 2 -> 0, of which waited for: 2 -> 0; matrix products, arithmetic and copies ran while one was open for 0% -> 0% of each run, Pallas kernels for 0% -> 0%
where the time goes in v1:
time: 761 us
  Pallas kernels  757 us (99%)
    pallas_call x1, Pallas kernels, per_device(): pl.pallas_call(functools.partial(kernel, v_tile), out_shape=(jax.ShapeDty...  757 us

profile of v1, /device:TPU:0, one launch (start us, length us, event | category | flops | bytes accessed | tf_op | source)
XLA Modules:
  0.0 760.6 jit_solution(4981276414094274785)
XLA Ops:
  0.6 757.4 %head.1 = (f32[16,128]{1,0:T(8,128)}, f32[16,128]{1,0:T(8,128)}, bf16[4,8192,1536]{2,1,0:T(8,128)(2,1)}) custom-call(bf16[2048,1536]{1,0:T(8,128)(2,1)} %h_ref.1, bf16[12608,1536]{1,0:T(8,128)(2,1)} %w_ref.1, s32[4,1,512]{2,1,0:T(1,128)} %bitcast.4, f32[16,128]{1,0:T(8,128)} %bitcast.5), custom_call_target="tpu_custom_call" | custom-call | tf_op jit(solution)/shard_map/head/pallas_call | solution.py:350
  758.0 1.3 copy.8
  759.3 1.3 copy.9

commit v2 on v1

--- a/solution.py
+++ b/solution.py
@@ -10,8 +10,10 @@
 MESH = pl.DeviceIdType.MESH
 SUBS = 4
 TILES = 16
-X_STEP = 34.0
-W_TIMES = (87.0, 174.0, 261.0, 382.0, 469.0, 522.0, 575.0, 620.0)
+FLOOR = float(jnp.finfo(jnp.float32).min)
+LINK_ORDER = ("H0", "H1", "W0", "W1", "W2", "F0", "F1", "H2", "H3", "W3", "W4", "F2", "F3", "W5", "W6", "W7")
+H_TIME, W_TIME, STEP_TIME, LAG = 33.7, 414.0, 2.8, 3.0
+MAX_RUN = 3
 
 
 def tile_of(q):
@@ -22,39 +24,107 @@
     return 3, q - 12
 
 
-def plan(n_chunks):
-    items = []
-    w_times = [W_TIMES[-1] * (j + 1) / n_chunks for j in range(n_chunks)] if n_chunks != len(W_TIMES) else W_TIMES
-    for q in range(TILES):
-        items.append((X_STEP * (q + 1), 0, ("x", q)))
-        items.append((X_STEP * (q + 1) + 4.0, 2, ("h", q)))
-    for i, t in enumerate((34.0, 121.0, 208.0, 329.0)):
-        items.append((t, 1, ("yz", i)))
-    for i, t in enumerate((330.0, 331.0, 416.0, 417.0)):
-        items.append((t, 1, ("diag", i)))
-    for j in range(n_chunks):
-        items.append((w_times[j], 3, ("w", j)))
-    items.sort()
-    runs, events, n_h, n_w = [], [], 0, 0
-    for _, _, (kind, k) in items:
-        events.append((kind, k))
-        if kind == "h":
-            if n_w:
-                runs.append((events, (k, 0, 0, 1, n_w)))
-                events = []
-            n_h += 1
-        if kind == "w":
-            if n_h:
-                runs.append((events, (0, 1, k, 0, n_h)))
-                events = []
-            n_w += 1
-    assert not events
-    return runs
+def link_order(n_chunks):
+    tokens = [(t[0], int(t[1:])) for t in LINK_ORDER]
+    last = max(k for kind, k in tokens if kind == "W")
+    tokens = [t for t in tokens if t[0] != "W" or t[1] < n_chunks] + [("W", j) for j in range(last + 1, n_chunks)]
+    start, after = [], [[], [], [], []]
+    current = start
+    for kind, k in tokens:
+        if kind == "F":
+            current = after[k // 2 * 2 + 1]
+        current.append((kind, k))
+    return start, after
+
+
+def stretches(values):
+    out, i = [], 0
+    while i < len(values):
+        n = 1
+        while n < MAX_RUN and i + n < len(values) and values[i + n] == values[i] + n:
+            n += 1
+        out.append((n, values[i]))
+        i += n
+    return out
+
+
+def plan(sizes):
+    start, after = link_order(len(sizes))
+    free, done, at = {"x": 0.0, "y": 0.0, "z": 0.0}, {}, {}
+    tiles, chunks, cells, runs, pending = [], [], set(), [], []
+    n_main = len(sizes) - 1
+
+    def put(link, token, now):
+        free[link] = max(free[link], now) + (W_TIME * sizes[token[1]] / sum(sizes) if token[0] == "W" else H_TIME)
+        done[link, token] = free[link]
+
+    def put_x(q, now):
+        put("x", ("X", q), now)
+        at["x", q] = free["x"] + LAG
+
+    def issue(token, now):
+        kind, k = token
+        for link in "yz" if kind != "F" else "yz"[k % 2]:
+            put(link, token, now)
+        if kind == "F":
+            at["diag", k] = done["yz"[k % 2], token] + LAG
+        else:
+            at["yz" if kind == "H" else "w", k] = max(done["y", token], done["z", token]) + LAG
+
+    def handle(e, now):
+        kind, k = e
+        del at[e]
+        pending.append(e)
+        if kind == "x":
+            at["h", k] = now + LAG
+        elif kind == "h":
+            tiles.append(k)
+        elif kind == "yz":
+            put_x(4 + 2 * k, now)
+            put_x(5 + 2 * k, now)
+            for token in after[k]:
+                issue(token, now)
+        elif kind == "diag":
+            put_x(12 + k, now)
+        elif k < n_main:
+            chunks.append(k)
+
+    def first():
+        return min(at, key=lambda e: (at[e], e))
+
+    for token in start:
+        issue(token, 0.0)
+    for q in range(4):
+        put_x(q, 0.0)
+    now = 0.0
+    while len(cells) < TILES * n_main:
+        while at and at[first()] <= now:
+            handle(first(), now)
+        options = [
+            (n, (q, 0, j, 1, n)) for q in sorted(tiles)
+            for n, j in stretches([j for j in sorted(chunks) if (q, j) not in cells])]
+        options += [
+            (n, (q, 1, j, 0, n)) for j in sorted(chunks)
+            for n, q in stretches([q for q in sorted(tiles) if (q, j) not in cells])]
+        if not options:
+            e = first()
+            now = max(now, at[e])
+            handle(e, now)
+            continue
+        _, run = max(options, key=lambda o: o[0])
+        q, dq, j, dj, n = run
+        cells.update((q + dq * i, j + dj * i) for i in range(n))
+        now += (n if runs else n - 1) * STEP_TIME
+        runs.append((pending[:], run))
+        pending.clear()
+    while at:
+        handle(first(), now)
+    return runs, pending
 
 
 def kernel(
     v_tile, h_ref, w_ref, ids_ref, q_ref, lp_ref, acc_ref, hbuf,
-    wv, hv, ids_all, mx, sm, pk, st_send, st_recv,
+    wv, hv, lg, lg_end, ids_all, mx, sm, pk, st_send, st_recv,
     ss, rs, wss, wrs, wls, iss, irs, ils, sss, srs, lsem,
 ):
     rows, kp = h_ref.shape
@@ -62,7 +132,9 @@
     vocab = w_ref.shape[0]
     share = vocab // 4
     n_chunks = -(-share // v_tile)
-    runs = plan(n_chunks)
+    sizes = [min(v_tile, share - j * v_tile) for j in range(n_chunks)]
+    runs, leftover = plan(sizes)
+    send_first, send_after = link_order(n_chunks)
 
     d, m = lax.axis_index("data"), lax.axis_index("model")
     y, z = lax.rem(d, 2), d // 2
@@ -95,25 +167,22 @@
             src_ref=hbuf.at[mm, pl.ds(row0(q), tile), :], dst_ref=hbuf.at[mm, pl.ds(row0(q), tile), :],
             send_sem=ss.at[0], recv_sem=rs.at[q * 4 + mm], device_id=(d, m), device_id_type=MESH).wait_recv()
 
-    def w_size(j):
-        return min(v_tile, share - j * v_tile)
-
     def send_w(j, rb):
-        size, dd = w_size(j), block(rb)
+        size, dd = sizes[j], block(rb)
         return pltpu.make_async_remote_copy(
             src_ref=w_ref.at[pl.ds(pl.multiple_of(dd * share + j * v_tile, 8), size), :],
             dst_ref=wv.at[pl.ds(j * v_tile, size), pl.ds(pl.multiple_of(d * kp, kp), kp)],
             send_sem=wss.at[j * 4 + rb], recv_sem=wrs.at[j * 4 + rb], device_id=(dd, m), device_id_type=MESH)
 
     def wait_w(j, rb):
-        size, dd = w_size(j), block(rb)
+        size, dd = sizes[j], block(rb)
         pltpu.make_async_remote_copy(
             src_ref=w_ref.at[pl.ds(0, size), :],
             dst_ref=wv.at[pl.ds(j * v_tile, size), pl.ds(pl.multiple_of(dd * kp, kp), kp)],
             send_sem=wss.at[j * 4 + rb], recv_sem=wrs.at[j * 4 + rb], device_id=(d, m), device_id_type=MESH).wait_recv()
 
     def local_w(j):
-        size = w_size(j)
+        size = sizes[j]
         return pltpu.make_async_copy(
             w_ref.at[pl.ds(pl.multiple_of(d * share + j * v_tile, 8), size), :],
             wv.at[pl.ds(j * v_tile, size), pl.ds(pl.multiple_of(d * kp, kp), kp)], wls.at[j])
@@ -123,16 +192,16 @@
             src_ref=ids_ref, dst_ref=ids_all.at[rb], send_sem=iss.at[rb], recv_sem=irs.at[rb],
             device_id=(block(rb), m), device_id_type=MESH)
 
-    def over_y(i):
-        send_h(own_piece(i), i, 4 + 2 * i, m, (block(1), m), 48 + i).start()
-
-    def over_z(i):
-        send_h(own_piece(i), i, 5 + 2 * i, m, (block(2), m), 52 + i).start()
-
-    def weights(j):
-        if j < n_chunks:
+    def put(kind, k):
+        if kind == "H":
+            send_h(own_piece(k), k, 4 + 2 * k, m, (block(1), m), 48 + k).start()
+            send_h(own_piece(k), k, 5 + 2 * k, m, (block(2), m), 52 + k).start()
+        elif kind == "F":
+            q = 5 + 2 * k if k % 2 == 0 else 4 + 2 * k
+            send_h(own_piece(q), q, 12 + k, m, (block(1 + k % 2), m), 56 + k).start()
+        else:
             for rb in (3, 1, 2):
-                send_w(j, rb).start()
+                send_w(k, rb).start()
 
     def spread(q):
         send_h(own_piece(q), q, q, m, (d, m_x), q).start()
@@ -148,21 +217,10 @@
         elif kind == "yz":
             wait_h(4 + 2 * k, m)
             wait_h(5 + 2 * k, m)
-            if k % 2 == 0:
-                send_h(own_piece(5 + 2 * k), 5 + 2 * k, 12 + k, m, (block(1), m), 56 + k).start()
-            else:
-                send_h(own_piece(4 + 2 * k), 4 + 2 * k, 12 + k, m, (block(2), m), 56 + k).start()
             spread(4 + 2 * k)
             spread(5 + 2 * k)
-            if k == 1:
-                over_y(3)
-                over_z(3)
-                weights(3)
-            elif k == 2:
-                weights(4)
-            elif k == 3:
-                for j in range(5, n_chunks):
-                    weights(j)
+            for token in send_after[k]:
+                put(*token)
         elif kind == "diag":
             wait_h(12 + k, m)
             spread(12 + k)
@@ -178,22 +236,26 @@
         sub = jnp.where(late, q - 12, jnp.where(mid, (q - 4) // 2, q))
         return rb, sub
 
-    def load_parts(q, slot, act):
+    def load_parts(q, slot):
         rb, sub = rb_sub(q)
         ry, rz = lax.rem(rb, 2), rb // 2
         yy, zz = y + ry - 2 * y * ry, z + rz - 2 * z * rz
         row = pl.multiple_of((zz * 2 + yy) * rows + sub * tile, tile)
-        for mm in range(4):
-            dst = hv.at[slot, :, pl.ds(mm * kp, kp)]
-            mine = jnp.logical_and(rb == 0, m == mm)
-
-            @pl.when(mine)
-            def _():
-                act(pltpu.make_async_copy(h_ref.at[pl.ds(pl.multiple_of(sub * tile, tile), tile), :], dst, lsem.at[slot * 4 + mm]))
-
-            @pl.when(jnp.logical_not(mine))
-            def _():
-                act(pltpu.make_async_copy(hbuf.at[mm, pl.ds(row, tile), :], dst, lsem.at[slot * 4 + mm]))
+
+        def part(mm, own):
+            src = h_ref.at[pl.ds(pl.multiple_of(sub * tile, tile), tile), :] if own else hbuf.at[mm, pl.ds(row, tile), :]
+            pltpu.make_async_copy(src, hv.at[slot, :, pl.ds(mm * kp, kp)], lsem.at[slot * 4 + mm]).start()
+
+        @pl.when(rb != 0)
+        def _():
+            for mm in range(4):
+                part(mm, False)
+
+        @pl.when(rb == 0)
+        def _():
+            for mm in range(4):
+                pl.when(m == mm)(functools.partial(part, mm, True))
+                pl.when(m != mm)(functools.partial(part, mm, False))
 
     def wait_parts(slot):
         for mm in range(4):
@@ -204,66 +266,69 @@
     own_ids.start()
     for rb in (1, 2, 3):
         send_ids(rb).start()
-    for i in range(3):
-        over_y(i)
-        over_z(i)
+    for i, token in enumerate(send_first):
+        put(*token)
         if i == 0:
             for q in range(4):
                 spread(q)
-        weights(i)
     for j in range(n_chunks):
         local_w(j).start()
-    mx[...] = jnp.full(mx.shape, -jnp.inf, jnp.float32)
+    mx[...] = jnp.full(mx.shape, FLOOR, jnp.float32)
     sm[...] = jnp.zeros(sm.shape, jnp.float32)
     pk[...] = jnp.zeros(pk.shape, jnp.float32)
+    lg[...] = jnp.full(lg.shape, -jnp.inf, jnp.float32)
+    lg_end[...] = jnp.full(lg_end.shape, -jnp.inf, jnp.float32)
     own_ids.wait()
     for rb in (1, 2, 3):
         send_ids(rb).wait()
 
-    first_events, first_run = runs[0]
-    for e in first_events:
+    base = m * vocab + d * share
+    nowhere = jnp.int32(1 << 30)
+
+    def product(start, size, slot):
+        return lax.dot_general(
+            wv[pl.ds(start, size), :], hv[slot], (((1,), (1,)), ((), ())), preferred_element_type=jnp.float32)
+
+    def absorb(ref, q, start):
+        rb, sub = rb_sub(q)
+        size = ref.shape[0]
+        spot = ids_all[rb, sub] - (base + start) - lax.broadcasted_iota(jnp.int32, (8, tile), 0)
+        old = mx[q]
+        new = old
+        for k in range(0, size, 8):
+            new = jnp.maximum(new, ref[k:k + 8, :])
+        grown, picked = sm[q] * jnp.exp(old - new), pk[q]
+        for k in range(0, size, 8):
+            part = ref[k:k + 8, :]
+            grown = grown + jnp.exp(part - new)
+            picked = picked + jnp.where(spot == k, part, 0.0)
+        mx[q] = new
+        sm[q] = grown
+        pk[q] = picked
+
+    n_runs = len(runs)
+    codes = []
+    for i, (_, (q0, dq, j0, dj, n)) in enumerate(runs):
+        q_next = runs[i + 1][1][0] if i + 1 < n_runs else 0
+        codes.append(((((q0 * 2 + dq) * 8 + j0) * 2 + dj) * 8 + n) * 16 + q_next)
+
+    for e in runs[0][0]:
         event(*e)
-    load_parts(jnp.int32(first_run[0]), 0, lambda c: c.start())
-
-    base = m * vocab + d * share
-
-    def compute(q, j, slot):
-        start = pl.multiple_of(jnp.minimum(j * v_tile, share - v_tile), 8)
-        skip = j * v_tile - start
-        logits = lax.dot_general(
-            wv[pl.ds(start, v_tile), :], hv[slot], (((1,), (1,)), ((), ())), preferred_element_type=jnp.float32)
-        local = lax.broadcasted_iota(jnp.int32, (v_tile, tile), 0)
-        fresh = local >= skip
-        rb, sub = rb_sub(q)
-        want = ids_all[rb, sub] - (base + start)
-        logits = jnp.where(fresh, logits, -jnp.inf)
-        hit = jnp.logical_and(fresh, local == want)
-        old = mx[q]
-        stack = logits.reshape(v_tile // 8, 8, tile)
-        new = jnp.maximum(old, jnp.max(stack, axis=0))
-        grown = jnp.sum(jnp.exp(stack - new[None]), axis=0)
-        sm[q] = sm[q] * jnp.exp(old - new) + grown
-        mx[q] = new
-        pk[q] = pk[q] + jnp.sum(jnp.where(hit, logits, 0.0).reshape(v_tile // 8, 8, tile), axis=0)
-
-    n_runs = len(runs)
-
-    def pick(r, values):
-        out = jnp.int32(values[0])
-        for i in range(1, len(values)):
-            if values[i] != values[i - 1]:
-                out = jnp.where(r >= i, jnp.int32(values[i]), out)
-        return out
-
-    q0s, dqs, j0s, djs, ns = (tuple(run[i] for _, run in runs) for i in range(5))
-
-    def run_body(r, s0):
-        q0, dq, j0, dj, n = (pick(r, v) for v in (q0s, dqs, j0s, djs, ns))
-        q_next = pick(r, q0s[1:] + (0,))
+    load_parts(jnp.int32(runs[0][1][0]), 0)
+
+    def run_body(r, carry):
+        code = jnp.int32(codes[0])
+        for i in range(1, n_runs):
+            code = jnp.where(r >= i, jnp.int32(codes[i]), code)
+        q_next, code = lax.rem(code, 16), code // 16
+        n, code = lax.rem(code, 8), code // 8
+        dj, code = lax.rem(code, 2), code // 2
+        j0, code = lax.rem(code, 8), code // 8
+        dq, q0 = lax.rem(code, 2), code // 2
 
         def step(i, carry):
-            s = s0 + i
-            slot = lax.rem(s, 2)
+            slot, fresh, q_old, start_old = carry
+            q = q0 + dq * i
             last = i == n - 1
 
             @pl.when(last)
@@ -275,18 +340,34 @@
                             for e in runs[k][0]:
                                 event(*e)
 
-            @pl.when(jnp.logical_not(jnp.logical_and(last, r == n_runs - 1)))
-            def _():
-                load_parts(jnp.where(last, q_next, q0 + dq * (i + 1)), 1 - slot, lambda c: c.start())
-
-            wait_parts(slot)
-            compute(q0 + dq * i, j0 + dj * i, slot)
-            return carry
-
-        lax.fori_loop(0, n, step, 0)
-        return s0 + n
-
-    lax.fori_loop(0, n_runs, run_body, jnp.int32(0))
+            q_new = jnp.where(last, q_next, q + dq)
+            pl.when(q_new != q)(lambda: load_parts(q_new, 1 - slot))
+            pl.when(fresh == 1)(lambda: wait_parts(slot))
+            start = pl.multiple_of((j0 + dj * i) * v_tile, 8)
+            absorb(lg, q_old, start_old)
+            lg[...] = product(start, v_tile, slot)
+            return jnp.where(q_new != q, 1 - slot, slot), jnp.where(q_new != q, 1, 0), q, start
+
+        return lax.fori_loop(0, n, step, carry)
+
+    zero = jnp.int32(0)
+    slot, fresh, q_old, start_old = lax.fori_loop(0, n_runs, run_body, (zero, jnp.int32(1), zero, nowhere))
+
+    absorb(lg, q_old, start_old)
+    for e in leftover:
+        event(*e)
+    end_start = (n_chunks - 1) * v_tile
+
+    def end_step(q, carry):
+        slot, fresh, q_old, start_old = carry
+        pl.when(q < TILES - 1)(lambda: load_parts(q + 1, 1 - slot))
+        pl.when(fresh == 1)(lambda: wait_parts(slot))
+        absorb(lg_end, q_old, start_old)
+        lg_end[...] = product(end_start, sizes[-1], slot)
+        return 1 - slot, jnp.int32(1), q, jnp.int32(end_start)
+
+    _, _, q_old, start_old = lax.fori_loop(0, TILES, end_step, (slot, fresh, zero, nowhere))
+    absorb(lg_end, q_old, start_old)
 
     lanes = 128
     for q in range(TILES):
@@ -359,6 +440,8 @@
             scratch_shapes=[
                 vmem((share, 4 * kp), jnp.bfloat16),
                 vmem((2, tile, 4 * kp), jnp.bfloat16),
+                vmem((v_tile, tile), jnp.float32),
+                vmem((share - (n_chunks - 1) * v_tile, tile), jnp.float32),
                 vmem((4, SUBS, 1, tile), jnp.int32),
                 vmem((TILES, 8, tile), jnp.float32),
                 vmem((TILES, 8, tile), jnp.float32),

time: 761 us -> 720 us (0.946)
  Pallas kernels: 757 us -> 716 us
    pallas_call x1, Pallas kernels: 757 us -> 716 us  [per_device(): pl.pallas_call(functools.partial(kernel, v_tile), out_shape=(jax.ShapeDty...]
where the time goes in v2:
time: 720 us
  Pallas kernels  716 us (99%)
    pallas_call x1, Pallas kernels, per_device(): pl.pallas_call(functools.partial(kernel, v_tile), out_shape=(jax.ShapeDty...  716 us

profile of v2, /device:TPU:0, one launch (start us, length us, event | category | flops | bytes accessed | tf_op | source)
XLA Modules:
  0.0 719.6 jit_solution(13713735081278534486)
XLA Ops:
  0.6 716.4 %head.1 = (f32[16,128]{1,0:T(8,128)}, f32[16,128]{1,0:T(8,128)}, bf16[4,8192,1536]{2,1,0:T(8,128)(2,1)}) custom-call(bf16[2048,1536]{1,0:T(8,128)(2,1)} %h_ref.1, bf16[12608,1536]{1,0:T(8,128)(2,1)} %w_ref.1, s32[4,1,512]{2,1,0:T(1,128)} %bitcast.4, f32[16,128]{1,0:T(8,128)} %bitcast.5), custom_call_target="tpu_custom_call" | custom-call | tf_op jit(solution)/shard_map/head/pallas_call | solution.py:431
  717.0 1.3 copy.8
  718.3 1.3 copy.9

commit v3 on v2

--- a/solution.py
+++ b/solution.py
@@ -12,7 +12,7 @@
 TILES = 16
 FLOOR = float(jnp.finfo(jnp.float32).min)
 LINK_ORDER = ("H0", "H1", "W0", "W1", "W2", "F0", "F1", "H2", "H3", "W3", "W4", "F2", "F3", "W5", "W6", "W7")
-H_TIME, W_TIME, STEP_TIME, LAG = 33.7, 414.0, 2.8, 3.0
+H_TIME, W_TIME, STEP_TIME, EARLY_TIME, LAG = 34.3, 422.0, 2.25, 8.0, 3.0
 MAX_RUN = 3
 
 
@@ -51,7 +51,7 @@
 def plan(sizes):
     start, after = link_order(len(sizes))
     free, done, at = {"x": 0.0, "y": 0.0, "z": 0.0}, {}, {}
-    tiles, chunks, cells, runs, pending = [], [], set(), [], []
+    tiles, chunks, cells, runs, pending, new = [], [], set(), [], [], []
     n_main = len(sizes) - 1
 
     def put(link, token, now):
@@ -78,7 +78,7 @@
         if kind == "x":
             at["h", k] = now + LAG
         elif kind == "h":
-            tiles.append(k)
+            new.append(k)
         elif kind == "yz":
             put_x(4 + 2 * k, now)
             put_x(5 + 2 * k, now)
@@ -97,35 +97,44 @@
     for q in range(4):
         put_x(q, 0.0)
     now = 0.0
+    last_step = 0.0
     while len(cells) < TILES * n_main:
-        while at and at[first()] <= now:
+        while at and at[first()] <= now and len(new) < 2:
             handle(first(), now)
         options = [
-            (n, (q, 0, j, 1, n)) for q in sorted(tiles)
+            (n, (0, q, 0, j, 1, n)) for q in sorted(tiles)
             for n, j in stretches([j for j in sorted(chunks) if (q, j) not in cells])]
         options += [
-            (n, (q, 1, j, 0, n)) for j in sorted(chunks)
+            (n, (0, q, 1, j, 0, n)) for j in sorted(chunks)
             for n, q in stretches([q for q in sorted(tiles) if (q, j) not in cells])]
-        if not options:
+        if new:
+            run = (1, new.pop(0), 0, 0, 0, 1)
+            tiles.append(run[1])
+            now += last_step
+            last_step = EARLY_TIME
+        elif options:
+            _, run = max(options, key=lambda o: o[0])
+            _, q, dq, j, dj, n = run
+            cells.update((q + dq * i, j + dj * i) for i in range(n))
+            now += last_step + (n - 1) * STEP_TIME
+            last_step = STEP_TIME
+        else:
             e = first()
             now = max(now, at[e])
             handle(e, now)
             continue
-        _, run = max(options, key=lambda o: o[0])
-        q, dq, j, dj, n = run
-        cells.update((q + dq * i, j + dj * i) for i in range(n))
-        now += (n if runs else n - 1) * STEP_TIME
         runs.append((pending[:], run))
         pending.clear()
+    now += last_step
     while at:
         handle(first(), now)
-    return runs, pending
+    return runs, pending, now
 
 
 def kernel(
-    v_tile, h_ref, w_ref, ids_ref, q_ref, lp_ref, acc_ref, hbuf,
-    wv, hv, lg, lg_end, ids_all, mx, sm, pk, st_send, st_recv,
-    ss, rs, wss, wrs, wls, iss, irs, ils, sss, srs, lsem,
+    v_tile, h_ref, w_ref, ids_ref, q_ref, lp_ref, acc_ref, hbuf, early,
+    wv, hv, he, staged, pin, lg, lg_end, ids_all, mx, sm, pk, st_send, st_recv,
+    ss, rs, wss, wrs, wls, iss, irs, ils, sss, srs, lsem, hsem, esem, psem,
 ):
     rows, kp = h_ref.shape
     tile = rows // SUBS
@@ -133,7 +142,7 @@
     share = vocab // 4
     n_chunks = -(-share // v_tile)
     sizes = [min(v_tile, share - j * v_tile) for j in range(n_chunks)]
-    runs, leftover = plan(sizes)
+    runs, leftover, _ = plan(sizes)
     send_first, send_after = link_order(n_chunks)
 
     d, m = lax.axis_index("data"), lax.axis_index("model")
@@ -171,21 +180,21 @@
         size, dd = sizes[j], block(rb)
         return pltpu.make_async_remote_copy(
             src_ref=w_ref.at[pl.ds(pl.multiple_of(dd * share + j * v_tile, 8), size), :],
-            dst_ref=wv.at[pl.ds(j * v_tile, size), pl.ds(pl.multiple_of(d * kp, kp), kp)],
+            dst_ref=wv.at[pl.ds(j * v_tile, size), pl.ds(rb * kp, kp)],
             send_sem=wss.at[j * 4 + rb], recv_sem=wrs.at[j * 4 + rb], device_id=(dd, m), device_id_type=MESH)
 
     def wait_w(j, rb):
-        size, dd = sizes[j], block(rb)
+        size = sizes[j]
         pltpu.make_async_remote_copy(
             src_ref=w_ref.at[pl.ds(0, size), :],
-            dst_ref=wv.at[pl.ds(j * v_tile, size), pl.ds(pl.multiple_of(dd * kp, kp), kp)],
+            dst_ref=wv.at[pl.ds(j * v_tile, size), pl.ds(rb * kp, kp)],
             send_sem=wss.at[j * 4 + rb], recv_sem=wrs.at[j * 4 + rb], device_id=(d, m), device_id_type=MESH).wait_recv()
 
     def local_w(j):
         size = sizes[j]
         return pltpu.make_async_copy(
             w_ref.at[pl.ds(pl.multiple_of(d * share + j * v_tile, 8), size), :],
-            wv.at[pl.ds(j * v_tile, size), pl.ds(pl.multiple_of(d * kp, kp), kp)], wls.at[j])
+            wv.at[pl.ds(j * v_tile, size), pl.ds(0, kp)], wls.at[j])
 
     def send_ids(rb):
         return pltpu.make_async_remote_copy(
@@ -214,6 +223,7 @@
         elif kind == "h":
             wait_h(k, m_sib)
             wait_h(k, m_xs)
+            load_piece(jnp.int32(k), 0, he.at[k % 2], hsem.at[k % 2])
         elif kind == "yz":
             wait_h(4 + 2 * k, m)
             wait_h(5 + 2 * k, m)
@@ -225,7 +235,6 @@
             wait_h(12 + k, m)
             spread(12 + k)
         else:
-            local_w(k).wait()
             for rb in (1, 2, 3):
                 wait_w(k, rb)
 
@@ -236,31 +245,36 @@
         sub = jnp.where(late, q - 12, jnp.where(mid, (q - 4) // 2, q))
         return rb, sub
 
-    def load_parts(q, slot):
+    def load_piece(q, part, dst, sem):
         rb, sub = rb_sub(q)
         ry, rz = lax.rem(rb, 2), rb // 2
         yy, zz = y + ry - 2 * y * ry, z + rz - 2 * z * rz
         row = pl.multiple_of((zz * 2 + yy) * rows + sub * tile, tile)
-
-        def part(mm, own):
-            src = h_ref.at[pl.ds(pl.multiple_of(sub * tile, tile), tile), :] if own else hbuf.at[mm, pl.ds(row, tile), :]
-            pltpu.make_async_copy(src, hv.at[slot, :, pl.ds(mm * kp, kp)], lsem.at[slot * 4 + mm]).start()
-
-        @pl.when(rb != 0)
+        mm = block(part)
+        mine = jnp.logical_and(rb == 0, mm == m)
+
+        @pl.when(mine)
         def _():
-            for mm in range(4):
-                part(mm, False)
-
-        @pl.when(rb == 0)
+            pltpu.make_async_copy(h_ref.at[pl.ds(pl.multiple_of(sub * tile, tile), tile), :], dst, sem).start()
+
+        @pl.when(jnp.logical_not(mine))
         def _():
-            for mm in range(4):
-                pl.when(m == mm)(functools.partial(part, mm, True))
-                pl.when(m != mm)(functools.partial(part, mm, False))
+            pltpu.make_async_copy(hbuf.at[mm, pl.ds(row, tile), :], dst, sem).start()
+
+    def load_parts(q, slot):
+        for part in (1, 2, 3):
+            load_piece(q, part, hv.at[slot, :, pl.ds((part - 1) * kp, kp)], lsem.at[slot * 4 + part])
 
     def wait_parts(slot):
-        for mm in range(4):
+        for part in (1, 2, 3):
             pltpu.make_async_copy(
-                h_ref.at[pl.ds(0, tile), :], hv.at[slot, :, pl.ds(mm * kp, kp)], lsem.at[slot * 4 + mm]).wait()
+                h_ref.at[pl.ds(0, tile), :], hv.at[slot, :, pl.ds((part - 1) * kp, kp)], lsem.at[slot * 4 + part]).wait()
+
+    def early_out(q, start, size, slot):
+        return pltpu.make_async_copy(staged.at[slot, pl.ds(0, size), :], early.at[q, pl.ds(start, size), :], esem.at[slot])
+
+    def early_in(q, start, size, slot):
+        return pltpu.make_async_copy(early.at[q, pl.ds(start, size), :], pin.at[slot, pl.ds(0, size), :], psem.at[slot])
 
     own_ids = pltpu.make_async_copy(ids_ref, ids_all.at[0], ils)
     own_ids.start()
@@ -281,13 +295,39 @@
     own_ids.wait()
     for rb in (1, 2, 3):
         send_ids(rb).wait()
+    for j in range(n_chunks):
+        local_w(j).wait()
 
     base = m * vocab + d * share
     nowhere = jnp.int32(1 << 30)
 
-    def product(start, size, slot):
-        return lax.dot_general(
-            wv[pl.ds(start, size), :], hv[slot], (((1,), (1,)), ((), ())), preferred_element_type=jnp.float32)
+    def dot(a, b):
+        return lax.dot_general(a, b, (((1,), (1,)), ((), ())), preferred_element_type=jnp.float32)
+
+    def product(start, size, slot, pslot):
+        return dot(wv[pl.ds(start, size), kp:], hv[slot]) + pin[pslot, :size]
+
+    end_start, end_size = (n_chunks - 1) * v_tile, sizes[-1]
+
+    def early_products(q):
+        half = lax.rem(q, 2)
+        pltpu.make_async_copy(h_ref.at[pl.ds(0, tile), :], he.at[half], hsem.at[half]).wait()
+
+        def one(j, carry):
+            slot = lax.rem(j, 2)
+            start = pl.multiple_of(j * v_tile, 8)
+            pl.when(j >= 2)(lambda: early_out(q, start, v_tile, slot).wait())
+            staged[slot] = dot(wv[pl.ds(start, v_tile), :kp], he[half])
+            early_out(q, start, v_tile, slot).start()
+            return carry
+
+        lax.fori_loop(0, n_chunks - 1, one, 0)
+        slot = (n_chunks - 1) % 2
+        early_out(q, 0, v_tile, slot).wait()
+        staged[slot, :end_size] = dot(wv[end_start:end_start + end_size, :kp], he[half])
+        early_out(q, end_start, end_size, slot).start()
+        early_out(q, 0, v_tile, 1 - slot).wait()
+        early_out(q, end_start, end_size, slot).wait()
 
     def absorb(ref, q, start):
         rb, sub = rb_sub(q)
@@ -307,28 +347,34 @@
         pk[q] = picked
 
     n_runs = len(runs)
-    codes = []
-    for i, (_, (q0, dq, j0, dj, n)) in enumerate(runs):
-        q_next = runs[i + 1][1][0] if i + 1 < n_runs else 0
-        codes.append(((((q0 * 2 + dq) * 8 + j0) * 2 + dj) * 8 + n) * 16 + q_next)
+    held, codes = TILES - 1, []
+    for i, (_, (kind, q0, dq, j0, dj, n)) in enumerate(runs):
+        following = runs[i + 1][1] if i + 1 < n_runs else (2, 0, 0, 0, 0, 1)
+        held = q0 + dq * (n - 1) if kind == 0 else held
+        q_next = held if following[0] == 1 else following[1]
+        held = q_next
+        code = 0
+        for digit, radix in (
+            (kind, 2), (q0, 16), (dq, 2), (j0, 8), (dj, 2), (n, 8), (q_next, 16), (following[3], 8), (following[0] == 0, 2)):
+            code = code * radix + int(digit)
+        codes.append(code)
 
     for e in runs[0][0]:
         event(*e)
-    load_parts(jnp.int32(runs[0][1][0]), 0)
 
     def run_body(r, carry):
         code = jnp.int32(codes[0])
         for i in range(1, n_runs):
             code = jnp.where(r >= i, jnp.int32(codes[i]), code)
-        q_next, code = lax.rem(code, 16), code // 16
-        n, code = lax.rem(code, 8), code // 8
-        dj, code = lax.rem(code, 2), code // 2
-        j0, code = lax.rem(code, 8), code // 8
-        dq, q0 = lax.rem(code, 2), code // 2
+        digits = []
+        for radix in (2, 8, 16, 8, 2, 8, 2, 16, 2):
+            digits.append(lax.rem(code, radix))
+            code = code // radix
+        next_main, j_next, q_next, n, dj, j0, dq, q0, kind = digits
 
         def step(i, carry):
-            slot, fresh, q_old, start_old = carry
-            q = q0 + dq * i
+            slot, fresh, held, pslot, q_old, start_old = carry
+            q, j = q0 + dq * i, j0 + dj * i
             last = i == n - 1
 
             @pl.when(last)
@@ -340,33 +386,57 @@
                             for e in runs[k][0]:
                                 event(*e)
 
-            q_new = jnp.where(last, q_next, q + dq)
-            pl.when(q_new != q)(lambda: load_parts(q_new, 1 - slot))
-            pl.when(fresh == 1)(lambda: wait_parts(slot))
-            start = pl.multiple_of((j0 + dj * i) * v_tile, 8)
-            absorb(lg, q_old, start_old)
-            lg[...] = product(start, v_tile, slot)
-            return jnp.where(q_new != q, 1 - slot, slot), jnp.where(q_new != q, 1, 0), q, start
+            q_new, j_new = jnp.where(last, q_next, q + dq), jnp.where(last, j_next, j + dj)
+            more = jnp.where(last, next_main, 1) == 1
+            after = pl.multiple_of(j_new * v_tile, 8)
+            start = pl.multiple_of(j * v_tile, 8)
+            pl.when(q_new != held)(lambda: load_parts(q_new, 1 - slot))
+
+            @pl.when(kind == 1)
+            def _():
+                early_products(q)
+                pl.when(more)(lambda: early_in(q_new, after, v_tile, pslot).start())
+
+            @pl.when(kind == 0)
+            def _():
+                pl.when(more)(lambda: early_in(q_new, after, v_tile, 1 - pslot).start())
+                pl.when(fresh == 1)(lambda: wait_parts(slot))
+                early_in(q, start, v_tile, pslot).wait()
+                absorb(lg, q_old, start_old)
+                lg[...] = product(start, v_tile, slot, pslot)
+
+            load = q_new != held
+            main = kind == 0
+            return (
+                jnp.where(load, 1 - slot, slot), jnp.where(load, 1, jnp.where(main, 0, fresh)), q_new,
+                jnp.where(main, 1 - pslot, pslot), jnp.where(main, q, q_old), jnp.where(main, start, start_old))
 
         return lax.fori_loop(0, n, step, carry)
 
     zero = jnp.int32(0)
-    slot, fresh, q_old, start_old = lax.fori_loop(0, n_runs, run_body, (zero, jnp.int32(1), zero, nowhere))
-
+    slot, fresh, _, pslot, q_old, start_old = lax.fori_loop(
+        0, n_runs, run_body, (zero, zero, jnp.int32(TILES - 1), zero, zero, nowhere))
+
+    early_in(0, end_start, end_size, pslot).start()
     absorb(lg, q_old, start_old)
     for e in leftover:
         event(*e)
-    end_start = (n_chunks - 1) * v_tile
 
     def end_step(q, carry):
-        slot, fresh, q_old, start_old = carry
-        pl.when(q < TILES - 1)(lambda: load_parts(q + 1, 1 - slot))
+        slot, fresh, pslot, q_old, start_old = carry
+
+        @pl.when(q < TILES - 1)
+        def _():
+            load_parts(q + 1, 1 - slot)
+            early_in(q + 1, end_start, end_size, 1 - pslot).start()
+
         pl.when(fresh == 1)(lambda: wait_parts(slot))
+        early_in(q, end_start, end_size, pslot).wait()
         absorb(lg_end, q_old, start_old)
-        lg_end[...] = product(end_start, sizes[-1], slot)
-        return 1 - slot, jnp.int32(1), q, jnp.int32(end_start)
-
-    _, _, q_old, start_old = lax.fori_loop(0, TILES, end_step, (slot, fresh, zero, nowhere))
+        lg_end[...] = product(end_start, end_size, slot, pslot)
+        return 1 - slot, jnp.int32(1), 1 - pslot, q, jnp.int32(end_start)
+
+    _, _, _, q_old, start_old = lax.fori_loop(0, TILES, end_step, (slot, fresh, pslot, zero, nowhere))
     absorb(lg_end, q_old, start_old)
 
     lanes = 128
@@ -428,18 +498,22 @@
         dma, vmem = pltpu.SemaphoreType.DMA, pltpu.VMEM
         any_space = pl.BlockSpec(memory_space=pl.ANY)
         in_vmem = pl.BlockSpec(memory_space=pltpu.VMEM)
-        lp, acc, _ = pl.pallas_call(
+        lp, acc, _, _ = pl.pallas_call(
             functools.partial(kernel, v_tile),
             out_shape=(
                 jax.ShapeDtypeStruct(flat, jnp.float32),
                 jax.ShapeDtypeStruct(flat, jnp.float32),
                 jax.ShapeDtypeStruct((4, 4 * rows, kp), jnp.bfloat16),
+                jax.ShapeDtypeStruct((TILES, share, tile), jnp.float32),
             ),
             in_specs=[any_space, any_space, in_vmem, in_vmem],
-            out_specs=(in_vmem, in_vmem, any_space),
+            out_specs=(in_vmem, in_vmem, any_space, any_space),
             scratch_shapes=[
                 vmem((share, 4 * kp), jnp.bfloat16),
-                vmem((2, tile, 4 * kp), jnp.bfloat16),
+                vmem((2, tile, 3 * kp), jnp.bfloat16),
+                vmem((2, tile, kp), jnp.bfloat16),
+                vmem((2, v_tile, tile), jnp.float32),
+                vmem((2, v_tile, tile), jnp.float32),
                 vmem((v_tile, tile), jnp.float32),
                 vmem((share - (n_chunks - 1) * v_tile, tile), jnp.float32),
                 vmem((4, SUBS, 1, tile), jnp.int32),
@@ -449,7 +523,7 @@
                 vmem((4, 3) + flat, jnp.float32),
                 vmem((16, 3) + flat, jnp.float32),
                 dma((60,)), dma((64,)), dma((4 * n_chunks,)), dma((4 * n_chunks,)), dma((n_chunks,)),
-                dma((4,)), dma((4,)), dma, dma((16,)), dma((16,)), dma((8,)),
+                dma((4,)), dma((4,)), dma, dma((16,)), dma((16,)), dma((8,)), dma((2,)), dma((2,)), dma((2,)),
             ],
             compiler_params=pltpu.CompilerParams(has_side_effects=True, vmem_limit_bytes=66_000_000),
             name="head",

time: 720 us -> 711 us (0.988)
  Pallas kernels: 716 us -> 707 us
    pallas_call x1, Pallas kernels: 716 us -> 707 us  [per_device(): pl.pallas_call(functools.partial(kernel, v_tile), out_shape=(jax.ShapeDty...]
where the time goes in v3:
time: 711 us
  Pallas kernels  707 us (99%)
    pallas_call x1, Pallas kernels, per_device(): pl.pallas_call(functools.partial(kernel, v_tile), out_shape=(jax.ShapeDty...  707 us

profile of v3, /device:TPU:0, one launch (start us, length us, event | category | flops | bytes accessed | tf_op | source)
XLA Modules:
  0.0 710.5 jit_solution(10354146511367027676)
XLA Ops:
  0.6 707.3 %head.1 = (f32[16,128]{1,0:T(8,128)}, f32[16,128]{1,0:T(8,128)}, bf16[4,8192,1536]{2,1,0:T(8,128)(2,1)}, f32[16,3152,512]{2,1,0:T(8,128)}) custom-call(bf16[2048,1536]{1,0:T(8,128)(2,1)} %h_ref.1, bf16[12608,1536]{1,0:T(8,128)(2,1)} %w_ref.1, s32[4,1,512]{2,1,0:T(1,128)} %bitcast.4, f32[16,128]{1,0:T(8,128)} %bitcast.5), custom_call_target="tpu_custom_call" | custom-call | tf_op jit(solution)/shard_map/head/pallas_call | solution.py:501
  707.9 1.3 copy.8
  709.2 1.3 copy.9

commit v4 on v3

--- a/solution.py
+++ b/solution.py
@@ -11,8 +11,8 @@
 SUBS = 4
 TILES = 16
 FLOOR = float(jnp.finfo(jnp.float32).min)
-LINK_ORDER = ("H0", "H1", "W0", "W1", "W2", "F0", "F1", "H2", "H3", "W3", "W4", "F2", "F3", "W5", "W6", "W7")
-H_TIME, W_TIME, STEP_TIME, EARLY_TIME, LAG = 34.3, 422.0, 2.25, 8.0, 3.0
+LINK_ORDER = ("H0", "W0", "W1", "H1", "W2", "H2", "F0", "F1", "W3", "H3", "W4", "F2", "F3", "W5", "W6", "W7")
+H_TIME, W_TIME, STEP_TIME, EARLY_TIME, LAG = 33.9, 417.0, 2.4, 8.7, 3.0
 MAX_RUN = 3
 
 
@@ -102,7 +102,7 @@
         while at and at[first()] <= now and len(new) < 2:
             handle(first(), now)
         options = [
-            (n, (0, q, 0, j, 1, n)) for q in sorted(tiles)
+            (n if n == 1 else n + 1.5, (0, q, 0, j, 1, n)) for q in sorted(tiles)
             for n, j in stretches([j for j in sorted(chunks) if (q, j) not in cells])]
         options += [
             (n, (0, q, 1, j, 0, n)) for j in sorted(chunks)
@@ -349,7 +349,7 @@
     n_runs = len(runs)
     held, codes = TILES - 1, []
     for i, (_, (kind, q0, dq, j0, dj, n)) in enumerate(runs):
-        following = runs[i + 1][1] if i + 1 < n_runs else (2, 0, 0, 0, 0, 1)
+        following = runs[i + 1][1] if i + 1 < n_runs else (2, TILES - 1, 0, 0, 0, 1)
         held = q0 + dq * (n - 1) if kind == 0 else held
         q_next = held if following[0] == 1 else following[1]
         held = q_next
@@ -417,49 +417,59 @@
     slot, fresh, _, pslot, q_old, start_old = lax.fori_loop(
         0, n_runs, run_body, (zero, zero, jnp.int32(TILES - 1), zero, zero, nowhere))
 
-    early_in(0, end_start, end_size, pslot).start()
+    lanes = 128
+    me = d * 4 + m
+
+    def finish(rb):
+        for q in [q for q in range(TILES) if tile_of(q)[0] == rb]:
+            sub = tile_of(q)[1]
+            old = mx[q]
+            top = jnp.max(old, axis=0, keepdims=True)
+            parts = (
+                top, jnp.sum(sm[q] * jnp.exp(old - top), axis=0, keepdims=True), jnp.sum(pk[q], axis=0, keepdims=True))
+            for k, part in enumerate(parts):
+                for i in range(tile // lanes):
+                    st_send[rb, k, pl.ds(sub * (tile // lanes) + i, 1), :] = part[:, i * lanes:(i + 1) * lanes]
+
+    def send_stats(rb, o):
+        return pltpu.make_async_remote_copy(
+            src_ref=st_send.at[rb], dst_ref=st_recv.at[me], send_sem=sss.at[rb * 4 + o], recv_sem=srs.at[me],
+            device_id=(block(rb), lax.rem(m + o, 4)), device_id_type=MESH)
+
+    others = [(rb, o) for rb in (3, 2, 1, 0) for o in range(4) if (rb, o) != (0, 0)]
+
+    def send_blocks(*blocks):
+        for rb, o in others:
+            if rb in blocks:
+                send_stats(rb, o).start()
+
+    early_in(TILES - 1, end_start, end_size, pslot).start()
     absorb(lg, q_old, start_old)
     for e in leftover:
         event(*e)
 
-    def end_step(q, carry):
+    def end_step(i, carry):
         slot, fresh, pslot, q_old, start_old = carry
-
-        @pl.when(q < TILES - 1)
+        q = TILES - 1 - i
+
+        @pl.when(q > 0)
         def _():
-            load_parts(q + 1, 1 - slot)
-            early_in(q + 1, end_start, end_size, 1 - pslot).start()
-
+            load_parts(q - 1, 1 - slot)
+            early_in(q - 1, end_start, end_size, 1 - pslot).start()
+
+        pl.when(q == 10)(lambda: finish(3))
+        pl.when(q == 9)(lambda: send_blocks(3))
+        pl.when(q == 2)(lambda: [finish(1), finish(2)] and None)
+        pl.when(q == 1)(lambda: send_blocks(2, 1))
         pl.when(fresh == 1)(lambda: wait_parts(slot))
         early_in(q, end_start, end_size, pslot).wait()
         absorb(lg_end, q_old, start_old)
         lg_end[...] = product(end_start, end_size, slot, pslot)
         return 1 - slot, jnp.int32(1), 1 - pslot, q, jnp.int32(end_start)
 
-    _, _, _, q_old, start_old = lax.fori_loop(0, TILES, end_step, (slot, fresh, pslot, zero, nowhere))
+    _, _, _, q_old, start_old = lax.fori_loop(0, TILES, end_step, (slot, fresh, pslot, jnp.int32(TILES - 1), nowhere))
     absorb(lg_end, q_old, start_old)
-
-    lanes = 128
-    for q in range(TILES):
-        rb, sub = tile_of(q)
-        old = mx[q]
-        top = jnp.max(old, axis=0, keepdims=True)
-        parts = (top, jnp.sum(sm[q] * jnp.exp(old - top), axis=0, keepdims=True), jnp.sum(pk[q], axis=0, keepdims=True))
-        for k, part in enumerate(parts):
-            for i in range(tile // lanes):
-                st_send[rb, k, pl.ds(sub * (tile // lanes) + i, 1), :] = part[:, i * lanes:(i + 1) * lanes]
-
-    me = d * 4 + m
-    st_recv[me] = st_send[0]
-
-    def send_stats(rb, o):
-        return pltpu.make_async_remote_copy(
-            src_ref=st_send.at[rb], dst_ref=st_recv.at[me], send_sem=sss.at[rb * 4 + o], recv_sem=srs.at[me],
-            device_id=(block(rb), lax.rem(m + o, 4)), device_id_type=MESH)
-
-    others = [(rb, o) for rb in (3, 2, 1, 0) for o in range(4) if (rb, o) != (0, 0)]
-    for rb, o in others:
-        send_stats(rb, o).start()
+    finish(0)
 
     def drain(i, carry):
         pltpu.make_async_remote_copy(
@@ -471,6 +481,8 @@
     for j in range(n_chunks):
         for rb in (1, 2, 3):
             send_w(j, rb).wait_send()
+    st_recv[me] = st_send[0]
+    send_blocks(0)
     for rb, o in others:
         send_stats(rb, o).wait_send()
     for rb, o in others:

time: 711 us -> 702 us (0.987)
  Pallas kernels: 707 us -> 696 us
    pallas_call x1, Pallas kernels: 707 us -> 696 us  [per_device(): pl.pallas_call(functools.partial(kernel, v_tile), out_shape=(jax.ShapeDty...]
where the time goes in v4:
time: 702 us; the launch traced here: 700 us
  Pallas kernels  696 us (99%)
    pallas_call x1, Pallas kernels, per_device(): pl.pallas_call(functools.partial(kernel, v_tile), out_shape=(jax.ShapeDty...  696 us

profile of v4, /device:TPU:0, one launch (start us, length us, event | category | flops | bytes accessed | tf_op | source)
XLA Modules:
  0.0 699.5 jit_solution(4977260216539275168)
XLA Ops:
  0.6 696.3 %head.1 = (f32[16,128]{1,0:T(8,128)}, f32[16,128]{1,0:T(8,128)}, bf16[4,8192,1536]{2,1,0:T(8,128)(2,1)}, f32[16,3152,512]{2,1,0:T(8,128)}) custom-call(bf16[2048,1536]{1,0:T(8,128)(2,1)} %h_ref.1, bf16[12608,1536]{1,0:T(8,128)(2,1)} %w_ref.1, s32[4,1,512]{2,1,0:T(1,128)} %bitcast.4, f32[16,128]{1,0:T(8,128)} %bitcast.5), custom_call_target="tpu_custom_call" | custom-call | tf_op jit(solution)/shard_map/head/pallas_call | solution.py:513
  696.9 1.3 copy.8
  698.2 1.3 copy.9

commit v5 on v4

--- a/solution.py
+++ b/solution.py
@@ -13,7 +13,8 @@
 FLOOR = float(jnp.finfo(jnp.float32).min)
 LINK_ORDER = ("H0", "W0", "W1", "H1", "W2", "H2", "F0", "F1", "W3", "H3", "W4", "F2", "F3", "W5", "W6", "W7")
 H_TIME, W_TIME, STEP_TIME, EARLY_TIME, LAG = 33.9, 417.0, 2.4, 8.7, 3.0
-MAX_RUN = 3
+CORE_LAG = 8.0
+MAX_RUN = 2
 
 
 def tile_of(q):
@@ -76,7 +77,7 @@
         del at[e]
         pending.append(e)
         if kind == "x":
-            at["h", k] = now + LAG
+            at["h", k] = now + CORE_LAG
         elif kind == "h":
             new.append(k)
         elif kind == "yz":
@@ -373,7 +374,7 @@
         next_main, j_next, q_next, n, dj, j0, dq, q0, kind = digits
 
         def step(i, carry):
-            slot, fresh, held, pslot, q_old, start_old = carry
+            slot, slot_1, slot_2, fresh, held, pslot, q_old, start_old = carry
             q, j = q0 + dq * i, j0 + dj * i
             last = i == n - 1
 
@@ -390,7 +391,8 @@
             more = jnp.where(last, next_main, 1) == 1
             after = pl.multiple_of(j_new * v_tile, 8)
             start = pl.multiple_of(j * v_tile, 8)
-            pl.when(q_new != held)(lambda: load_parts(q_new, 1 - slot))
+            load = q_new != held
+            pl.when(load)(lambda: load_parts(q_new, slot_1))
 
             @pl.when(kind == 1)
             def _():
@@ -405,17 +407,18 @@
                 absorb(lg, q_old, start_old)
                 lg[...] = product(start, v_tile, slot, pslot)
 
-            load = q_new != held
             main = kind == 0
             return (
-                jnp.where(load, 1 - slot, slot), jnp.where(load, 1, jnp.where(main, 0, fresh)), q_new,
+                jnp.where(load, slot_1, slot), jnp.where(load, slot_2, slot_1), jnp.where(load, slot, slot_2),
+                jnp.where(load, 1, jnp.where(main, 0, fresh)), q_new,
                 jnp.where(main, 1 - pslot, pslot), jnp.where(main, q, q_old), jnp.where(main, start, start_old))
 
         return lax.fori_loop(0, n, step, carry)
 
     zero = jnp.int32(0)
-    slot, fresh, _, pslot, q_old, start_old = lax.fori_loop(
-        0, n_runs, run_body, (zero, zero, jnp.int32(TILES - 1), zero, zero, nowhere))
+    one, two = jnp.int32(1), jnp.int32(2)
+    slot, slot_1, slot_2, fresh, _, pslot, q_old, start_old = lax.fori_loop(
+        0, n_runs, run_body, (zero, one, two, zero, jnp.int32(TILES - 1), zero, zero, nowhere))
 
     lanes = 128
     me = d * 4 + m
@@ -443,18 +446,19 @@
             if rb in blocks:
                 send_stats(rb, o).start()
 
+    load_parts(jnp.int32(TILES - 2), slot_1)
     early_in(TILES - 1, end_start, end_size, pslot).start()
     absorb(lg, q_old, start_old)
     for e in leftover:
         event(*e)
 
     def end_step(i, carry):
-        slot, fresh, pslot, q_old, start_old = carry
+        slot, slot_1, slot_2, fresh, pslot, q_old, start_old = carry
         q = TILES - 1 - i
+        pl.when(q > 1)(lambda: load_parts(q - 2, slot_2))
 
         @pl.when(q > 0)
         def _():
-            load_parts(q - 1, 1 - slot)
             early_in(q - 1, end_start, end_size, 1 - pslot).start()
 
         pl.when(q == 10)(lambda: finish(3))
@@ -465,9 +469,10 @@
         early_in(q, end_start, end_size, pslot).wait()
         absorb(lg_end, q_old, start_old)
         lg_end[...] = product(end_start, end_size, slot, pslot)
-        return 1 - slot, jnp.int32(1), 1 - pslot, q, jnp.int32(end_start)
-
-    _, _, _, q_old, start_old = lax.fori_loop(0, TILES, end_step, (slot, fresh, pslot, jnp.int32(TILES - 1), nowhere))
+        return slot_1, slot_2, slot, jnp.int32(1), 1 - pslot, q, jnp.int32(end_start)
+
+    *_, q_old, start_old = lax.fori_loop(
+        0, TILES, end_step, (slot, slot_1, slot_2, fresh, pslot, jnp.int32(TILES - 1), nowhere))
     absorb(lg_end, q_old, start_old)
     finish(0)
 
@@ -522,7 +527,7 @@
             out_specs=(in_vmem, in_vmem, any_space, any_space),
             scratch_shapes=[
                 vmem((share, 4 * kp), jnp.bfloat16),
-                vmem((2, tile, 3 * kp), jnp.bfloat16),
+                vmem((3, tile, 3 * kp), jnp.bfloat16),
                 vmem((2, tile, kp), jnp.bfloat16),
                 vmem((2, v_tile, tile), jnp.float32),
                 vmem((2, v_tile, tile), jnp.float32),
@@ -535,9 +540,9 @@
                 vmem((4, 3) + flat, jnp.float32),
                 vmem((16, 3) + flat, jnp.float32),
                 dma((60,)), dma((64,)), dma((4 * n_chunks,)), dma((4 * n_chunks,)), dma((n_chunks,)),
-                dma((4,)), dma((4,)), dma, dma((16,)), dma((16,)), dma((8,)), dma((2,)), dma((2,)), dma((2,)),
+                dma((4,)), dma((4,)), dma, dma((16,)), dma((16,)), dma((12,)), dma((2,)), dma((2,)), dma((2,)),
             ],
-            compiler_params=pltpu.CompilerParams(has_side_effects=True, vmem_limit_bytes=66_000_000),
+            compiler_params=pltpu.CompilerParams(has_side_effects=True, vmem_limit_bytes=67_043_328),
             name="head",
         )(h_part, w_part, draft_loc.reshape(SUBS, 1, tile), q_loc.reshape(flat))
         return lp.reshape(rows), acc.reshape(rows)

time: 702 us -> 710 us (1.011)
  Pallas kernels: 696 us -> 704 us
    pallas_call x1, Pallas kernels: 696 us -> 704 us  [per_device(): pl.pallas_call(functools.partial(kernel, v_tile), out_shape=(jax.ShapeDty...]
where the time goes in v5:
time: 710 us; the launch traced here: 707 us
  Pallas kernels  704 us (99%)
    pallas_call x1, Pallas kernels, per_device(): pl.pallas_call(functools.partial(kernel, v_tile), out_shape=(jax.ShapeDty...  704 us

profile of v5, /device:TPU:0, one launch (start us, length us, event | category | flops | bytes accessed | tf_op | source)
XLA Modules:
  0.0 707.4 jit_solution(7431315992411959660)
XLA Ops:
  0.6 704.2 %head.1 = (f32[16,128]{1,0:T(8,128)}, f32[16,128]{1,0:T(8,128)}, bf16[4,8192,1536]{2,1,0:T(8,128)(2,1)}, f32[16,3152,512]{2,1,0:T(8,128)}) custom-call(bf16[2048,1536]{1,0:T(8,128)(2,1)} %h_ref.1, bf16[12608,1536]{1,0:T(8,128)(2,1)} %w_ref.1, s32[4,1,512]{2,1,0:T(1,128)} %bitcast.4, f32[16,128]{1,0:T(8,128)} %bitcast.5), custom_call_target="tpu_custom_call" | custom-call | tf_op jit(solution)/shard_map/head/pallas_call | solution.py:518
  704.9 1.3 copy.8
  706.1 1.3 copy.9
